TPU v7x, 32 devices: a whole 2x2x4 slice. The times are simulated.
32 devices in a mesh: dp: 8 (over y, x, core), tensor: 4 (over z).
Axes of the slice: x: 2, y: 2, z: 4, core: 2. Of those that a mesh axis runs over, the one named last changes fastest.
Arguments:
- hidden_in: bfloat16 [4096, 2048], P('dp', 'tensor'), may hold values from -6 to 6
- cotangent: bfloat16 [4096, 2048], P('dp', 'tensor'), may hold values from -6 to 6
- segment_ids: int32 [4096], P('dp'), may hold values from -1 to 4095, as said below
- positions: int32 [4096], P('dp'), may hold values from 0 to 1023, as said below
- norm_gain: float32 [2048], replicated, may hold values from 0.25 to 1.75
- norm_shift: float32 [2048], replicated, may hold values from -1.5 to 1.5
- qkv_weight: bfloat16 [2048, 3, 2048], P(None, None, 'tensor'), may hold values from -0.53033009 to 0.53033009
- qv_bias: float32 [2, 2048], P(None, 'tensor'), may hold values from -3 to 3
- key_bias: float32 [32, 32], P('tensor'), may hold values from -3 to 3
- dense_weight: bfloat16 [2048, 2048], P('tensor'), may hold values from -1.5 to 1.5
- fc1_weight: bfloat16 [2048, 8192], P(None, 'tensor'), may hold values from -0.125 to 0.125
- fc1_bias: float32 [8192], P('tensor'), may hold values from -3 to 3
- fc2_weight: bfloat16 [8192, 2048], P('tensor'), may hold values from -0.0625 to 0.0625
- out_bias: float32 [2, 2048], replicated, may hold values from -1.5 to 1.5
Outputs:
- block_out: bfloat16 [4096, 2048], P('dp', 'tensor')
- input_grad: float32 [4096, 2048], P('dp', 'tensor')
- norm_grad: float32 [2, 2048], P(None, ('tensor', 'dp'))
- qkv_grad: float32 [2048, 3, 2048], P('dp', None, 'tensor')
- qvbias_grad: float32 [2, 2048], P(None, ('tensor', 'dp'))
- keybias_grad: float32 [32, 32], P('tensor', 'dp')
- dense_grad: float32 [2048, 2048], P(('tensor', 'dp'))
- fc1_grad: float32 [2048, 8192], P('dp', 'tensor')
- fc1bias_grad: float32 [8192], P(('tensor', 'dp'))
- fc2_grad: float32 [8192, 2048], P(('tensor', 'dp'))
- outbias_grad: float32 [2, 2048], P(None, ('tensor', 'dp'))
Inputs may be any that keep to these rules, and one draw needn't show every extreme that they name: `segment_ids`: the tokens of one segment id stand in a row inside one block of 512 slots, and different segments have different ids; -1 marks unused slots, which end a block; every block has 256 or more used slots, and some block is a single segment of 512 tokens. Within a segment the positions rise by one from token to token; unused slots have position 0.
All inputs are finite; a program needn't handle non-finite values.
Results may differ from a plain program's by a relative error of at most 0.028.
The roundings to bfloat16 on the way count: a program that leaves them out, or rounds other values in their place, can miss the bound.
Values may be sent and summed in bfloat16 or wider, within the bound.
A program may use at most 256 MiB of HBM per device.

v0:
```python
import functools

import jax
import jax.numpy as jnp
import numpy as np
from jax import lax
from jax.experimental import pallas as pl
from jax.experimental.pallas import tpu as pltpu
from jax.sharding import PartitionSpec as P

HD = 64
ROT = 32
LANES = 128

norm_epsilon = 1e-05
gelu_scale = 0.7978845608028654
gelu_cubic = 0.044715
masked_score = -1e30

MESH = pl.DeviceIdType.MESH
F32 = jnp.float32
BF16 = jnp.bfloat16
VMEM_BYTES = 67043328


def gelu_tanh(u):
    return jnp.tanh(u * (gelu_scale + (gelu_scale * gelu_cubic) * (u * u)))


def gelu_slope(u):
    tanh_val = gelu_tanh(u)
    return 0.5 * (1.0 + tanh_val) + (0.5 * u) * (1.0 - tanh_val * tanh_val) * (
        gelu_scale + (3.0 * gelu_scale * gelu_cubic) * (u * u)
    )


class Place:
    def __init__(self, nd, nt):
        self.nd, self.nt = nd, nt
        self.nch = nd // 2
        self.bits = self.nch.bit_length() - 1
        self.d = lax.axis_index("dp")
        self.t = lax.axis_index("tensor")
        self.c = lax.rem(self.d, 2)
        self.j = self.d // 2

    def pair(self):
        return (self.d + 1 - 2 * self.c, self.t)

    def chip_bit(self, b):
        return lax.rem(self.j // (1 << b), 2)

    def over(self, b):
        step = 2 << b
        return (self.d + step - 2 * step * self.chip_bit(b), self.t)

    def right(self):
        return (self.d, jnp.minimum(self.t + 1, self.nt - 1))

    def left(self):
        return (self.d, jnp.maximum(self.t - 1, 0))


def remote(src, dst, send, recv, device):
    return pltpu.make_async_remote_copy(
        src_ref=src, dst_ref=dst, send_sem=send, recv_sem=recv, device_id=device, device_id_type=MESH
    )


def greet(place):
    barrier = pltpu.get_barrier_semaphore()

    def signal(d, t):
        pl.semaphore_signal(barrier, inc=1, device_id=(d, t), device_id_type=MESH)

    for k in range(1, place.nd):
        signal(lax.rem(place.d + k, place.nd), place.t)
    for k in range(1, place.nt):
        signal(place.d, lax.rem(place.t + k, place.nt))
        signal(place.pair()[0], lax.rem(place.t + k, place.nt))


def greeted(place):
    pl.semaphore_wait(pltpu.get_barrier_semaphore(), place.nd - 1 + 2 * (place.nt - 1))


BK = 512
TW = 256


def mm(a, b, ca=1, cb=0):
    return lax.dot_general(a, b, (((ca,), (cb,)), ((), ())), preferred_element_type=F32)


def cat(parts, axis):
    return jnp.concatenate(parts, axis=axis)


def at512(i):
    return pl.ds(pl.multiple_of(i * BK, BK), BK)


def at256(i):
    return pl.ds(pl.multiple_of(i * TW, TW), TW)


class Plan:
    def __init__(self, nd, nt, units, heads, ub):
        self.nd, self.nt = nd, nt
        self.nch = nd // 2
        self.bits = self.nch.bit_length() - 1
        self.units, self.heads, self.ub = units, heads, ub
        self.hw = heads * HD
        self.nu = units // BK
        self.width = nt * BK
        self.rb = self.width // nd
        self.rd = 2 * self.hw // nd
        n = 0
        for name, size in (
            ("xb", 2 * nt),
            ("cb", 2 * nt),
            ("hb", 2 * nt),
            ("w1b", 2 * nt + 1),
            ("w2b", 2 * nt + 1),
            ("f2b", self.nu * nt),
            ("f1b", self.nu * nt),
            ("xo", 1),
            ("co", 1),
        ):
            setattr(self, name, n)
            n += size
        self.blocks = n
        self.n2 = 2 * nt
        self.n1 = 2 * (units // TW)
        self.n3 = 2 * 3
        self.pieces = self.n2 + self.n1 + self.n3 + nt


class Piece:
    def __init__(self, place, order, view, recv, ss, rs):
        self.p, self.order, self.view, self.r, self.ss, self.rs = place, order, view, recv, ss, rs
        self.off = [0]
        for i in range(len(order)):
            self.off.append(self.off[-1] + (place.nch >> (i + 1)))

    def block(self, i, m, mine):
        j = 0
        for b in self.order[:i]:
            j = j + self.p.chip_bit(b) * (1 << b)
        if i < len(self.order):
            b = self.order[i]
            v = self.p.chip_bit(b)
            j = j + (v if mine else 1 - v) * (1 << b)
            for q, b2 in enumerate(self.order[i + 1 :]):
                j = j + ((m >> q) & 1) * (1 << b2)
        return j

    def held(self, i, m, before):
        idx = 0
        for r in range(before + 1, min(i, len(self.order))):
            idx = idx + self.p.chip_bit(self.order[r]) * (1 << (r - before - 1))
        if i < len(self.order):
            v = self.p.chip_bit(self.order[i])
            idx = idx + (1 - v) * (1 << (i - before - 1)) + m * (1 << (i - before))
        return self.off[before] + idx

    def copy(self, i, m):
        k = self.off[i] + m
        return remote(
            self.view(self.block(i, m, False)),
            self.r.at[k],
            self.ss.at[k],
            self.rs.at[k],
            self.p.over(self.order[i]),
        )

    def total(self, i, m, rows):
        acc = self.view(self.block(i, m, False))[rows, :].astype(F32)
        for before in range(i):
            acc = acc + self.r[self.held(i, m, before), rows, :].astype(F32)
        return acc

    def each(self, do):
        rows = self.view(0).shape[0]
        size = min(rows, 64)

        @pl.loop(0, rows // size)
        def _(q):
            do(pl.ds(pl.multiple_of(q * size, size), size))

    def start(self, i):
        for m in range(self.p.nch >> (i + 1)):
            if i > 0:
                dst = self.view(self.block(i, m, False))

                def put(rows, dst=dst, m=m):
                    dst[rows, :] = self.total(i, m, rows).astype(BF16)

                self.each(put)
            self.copy(i, m).start()

    def wait(self, i):
        for m in range(self.p.nch >> (i + 1)):
            self.copy(i, m).wait()

    def final(self, to):
        def put(rows):
            to[rows, :] = self.total(len(self.order), 0, rows).astype(to.dtype)

        self.each(put)


def block_kernel(pn, direct, *refs):
    (
        x_in, c_in, seg_in, pos_in, freq, gain, shift, w1, w2, wq, wd, b1, qvb, kb, obias,
        block_out, input_grad, norm_out, qkv_out, qvb_out, keyb_out, dense_out, fc1_out, fc1b_out,
        fc2_out, outb_out,
        pool, wq_v, wd_v, tab, segr, act, buf, pre_v, qkv, attn, attn_p, dl, at_tmp, dg, dr, rp, fs, fr,
        ostage, mi, bias3, fb, ob, ng, sv, rv, stc, stt, sr, st, kbv,
        s_load, s_z, r_z, s_c, r_c, s_tab, s_p, r_p, s_d, r_d, s_f, s_os, s_a, s_oc, r_oc, s_ol, r_ol,
        s_hc, r_hc, s_hl, r_hl, s_v, r_v, s_s, r_s, s_st, r_st, credit,
    ) = refs
    nd, nt, nch, nu = pn.nd, pn.nt, pn.nch, pn.nu
    hw, ub, rb, rd = pn.hw, pn.ub, pn.rb, pn.rd
    place = Place(nd, nt)
    t, c, d = place.t, place.c, place.d
    nq = pn.units // TW

    def load(i, src, dst):
        return pltpu.make_async_copy(src, dst, s_load.at[i])

    loads = {
        "x": [load(0, x_in, pool.at[pn.xb + t])],
        "c": [load(1, c_in, pool.at[pn.cb + t])],
        "wd": [load(4, wd.at[pl.ds(pl.multiple_of(c * hw, hw), hw), :], wd_v)],
        "wq": [
            load(5, wq.at[:, :, pl.ds(pl.multiple_of(c * hw, hw), hw)], wq_v)
        ],
        "xo": [load(8, x_in, pool.at[pn.xo]), load(9, c_in, pool.at[pn.co])],
        "w1": [],
        "w2": [],
        "w1r": [],
    }
    n = 10
    for q in range(nq):
        col = (2 * q + c if direct else q) * TW
        src = w1.at[:, :, pl.ds(pl.multiple_of(col, TW), TW)]
        half = pl.ds((q % 2) * TW, TW)
        loads["w1"].append(load(n, src, pool.at[pl.ds(pn.w1b + (q // 2) * nt, nt), :, half]))
        loads["w1r"].append(load(n + 1, src, pool.at[pl.ds(pn.cb + (q // 2) * nt, nt), :, half]))
        n += 2
        for k in range(nt):
            src = w2.at[pl.ds(pl.multiple_of(col, TW), TW), pl.ds(k * BK, BK)]
            loads["w2"].append(load(n, src, pool.at[pn.w2b + (q // 2) * nt + k, half, :]))
            n += 1

    def begin(*names):
        for name in names:
            for cp in loads[name]:
                cp.start()

    def arrive(*names):
        for name in names:
            for cp in loads[name]:
                cp.wait()

    begin("x", "c", "w1", "wq", "wd", "w2", "xo")
    greet(place)
    arrive("x")

    first = lax.broadcasted_iota(jnp.int32, (64, LANES), 1) == 0

    @pl.loop(0, BK // 64)
    def _(q):
        rows = pl.ds(pl.multiple_of(q * 64, 64), 64)
        v = pool[pn.xb + t, rows, :].astype(F32)
        m = jnp.sum(v, axis=1, keepdims=True) / BK
        v = v - m
        stc[rows, :] = jnp.where(first, m, jnp.sum(v * v, axis=1, keepdims=True))

    stt[...] = stc[...].T[:8]
    greeted(place)

    def blk(a, s, k, f):
        return pool.at[a * (pn.cb - pn.xb) + pn.xb + s * nt + k, at256(f), :]

    def z_dev(side):
        return place.right() if side == 0 else place.left()

    def z_copy(a, k, side, f):
        return remote(blk(a, 0, k, f), blk(a, 0, k, f), s_z.at[side, a, k, f], r_z.at[a, k, f], z_dev(side))

    def c_copy(a, k, f):
        return remote(blk(a, 0, k, f), blk(a, 1, k, f), s_c.at[a, k, f], r_c.at[a, k, f], place.pair())

    def own_z(a, side, f):
        src = (x_in, c_in)[a].at[at256(f), :]
        return remote(src, blk(a, 0, t, f), s_z.at[side, a, t, f], r_z.at[a, t, f], z_dev(side))

    def own_c(a, f):
        src = (x_in, c_in)[a].at[at256(f), :]
        return remote(src, blk(a, 1, t, f), s_c.at[a, t, f], r_c.at[a, t, f], place.pair())

    def tab_copies():
        return (
            remote(tab.at[0], tab.at[1], s_tab.at[0], s_tab.at[1], place.pair()),
            remote(segr.at[0], segr.at[1], s_tab.at[2], s_tab.at[3], place.pair()),
        )

    def item(side, who, i):
        if side == 0:
            first = i <= who
            return jnp.where(first, 0, 1), jnp.where(first, who - i, 2 * who + 1 - i)
        m = nt - who
        first = i < m
        return jnp.where(first, 0, 1), jnp.where(first, who + i, who + i - m)

    def progress(step, halves=(0, 1)):
        for f in halves:
            if step >= 1:
                @pl.when((t > 0) & (step - 1 < 2 * t))
                def _():
                    a, k = item(0, t - 1, step - 1)
                    z_copy(a, k, 0, f).wait_recv()
                    c_copy(a, k, f).start()

                @pl.when((t < nt - 1) & (step - 1 < 2 * (nt - 1 - t)))
                def _():
                    a, k = item(1, t + 1, step - 1)
                    z_copy(a, k, 1, f).wait_recv()
                    c_copy(a, k, f).start()

            for side in range(2):
                me = t if side == 0 else nt - 1 - t
                if step == 0:
                    pl.when(me < nt - 1)(lambda side=side: own_z(0, side, f).start())
                else:
                    @pl.when((me < nt - 1) & (step <= me))
                    def _():
                        z_copy(0, me - step if side == 0 else nt - 1 - me + step, side, f).start()

                @pl.when((me < nt - 1) & (step > me) & (step <= 2 * me))
                def _():
                    k = 2 * me - step
                    z_copy(1, k if side == 0 else nt - 1 - k, side, f).start()

        for side in range(2 if 1 in halves else 0):
            me = t if side == 0 else nt - 1 - t

            @pl.when((me < nt - 1) & (step == me))
            def _():
                own_z(1, side, 0).start()
                own_z(1, side, 1).start()

    def z_sent(a):
        for f in range(2):
            for m in range(nt):
                for side in range(2):
                    me = t if side == 0 else nt - 1 - t

                    @pl.when((me < nt - 1) & (m <= me))
                    def _():
                        k = me - m
                        z_copy(a, k if side == 0 else nt - 1 - k, side, f).wait_send()

            for k in range(nt):
                c_copy(a, k, f).wait_send()

    def arrival(tt, k):
        if k == tt:
            return -1
        return 2 * tt - 1 - k if k < tt else (nt - 1 - tt) + (k - tt - 1)

    orders = [sorted(range(nt), key=lambda k, tt=tt: (arrival(tt, k), k)) for tt in range(nt)]
    needed = [max(arrival(tt, orders[tt][i]) for tt in range(nt)) + 1 for i in range(nt)]

    def chunk(i):
        k = orders[0][i]
        for tt in range(1, nt):
            k = jnp.where(t == tt, orders[tt][i], k)
        return k

    def st_copy(s, k):
        peer = lax.rem(t + k, nt)
        dev = (d, peer) if s == 0 else (place.pair()[0], peer)
        return remote(stt, st.at[s, t], s_st.at[s, k], r_st.at[s, t], dev)

    for k in range(nt):
        for s in range(2):
            if k or s:
                st_copy(s, k).start()
    progress(0)
    for f in range(2):
        own_c(0, f).start()
    st[0, t] = stt[...]

    def column(row):
        return jnp.broadcast_to(row.astype(F32), (LANES, BK)).T

    lane1 = lax.broadcasted_iota(jnp.int32, (1, LANES), 1)
    dim1 = lax.rem(lane1, HD)
    angles = column(pos_in[...]) * freq[...]
    tab[0, :, pl.ds(0, LANES)] = jnp.where(dim1 < ROT, jnp.cos(angles), 1.0)
    sine = jnp.sin(angles)
    sine = jnp.where(dim1 < ROT // 2, -sine, sine)
    tab[0, :, pl.ds(LANES, LANES)] = jnp.where(dim1 < ROT, sine, 0.0)
    tab[0, :, pl.ds(2 * LANES, LANES)] = column(seg_in[...])
    segr[0] = jnp.broadcast_to(seg_in[...].astype(F32), (8, BK))
    kbv[...] = jnp.zeros_like(kbv)
    for h in range(pn.heads):
        kbv[pl.ds(0, 1), pl.ds(h * HD, ROT)] = kb[pl.ds(c * pn.heads + h, 1), :]
    arrive("c")
    for f in range(2):
        own_c(1, f).start()
    for cp in tab_copies():
        cp.start()
    fb[...] = jnp.zeros_like(fb)
    bias3[...] = jnp.zeros_like(bias3)
    ng[...] = jnp.zeros_like(ng)
    for k in range(nt):
        for s in range(2):
            if k or s:
                frm = lax.rem(t + k, nt)
                st_copy(s, k).wait_send()
                remote(stt, st.at[s, frm], s_st.at[s, k], r_st.at[s, frm], place.pair()).wait_recv()
    for s in range(2):
        mean = sum(st[s, k, pl.ds(0, 1), :] for k in range(nt)) / nt
        dev = 0.0
        for k in range(nt):
            off = st[s, k, pl.ds(0, 1), :] - mean
            dev = dev + st[s, k, pl.ds(1, 1), :] + BK * off * off
        inv = lax.rsqrt(dev / pn.width + norm_epsilon)
        both = jnp.concatenate([mean, inv, jnp.zeros((LANES - 2, BK), F32)], axis=0)
        mi[s] = both.T
    arrive("w1")

    def live(s):
        return tab[s, :, pl.ds(2 * LANES, 1)] >= 0.0

    def gelu_block(s, u, pre):
        bias = []
        for q in range(2):
            col = (2 * (2 * u + q) + c if direct else 2 * u + q) * TW
            bias.append(b1[:, pl.ds(pl.multiple_of(col, TW), TW)])
        pre = pre + cat(bias, 1)
        val = (0.5 * pre * (1.0 + gelu_tanh(pre))).astype(BF16)
        act[s, :, at512(u)] = val
        val = jnp.where(live(s), val, jnp.zeros_like(val))
        buf[at512(u), at512(s)] = val.T

    def take(k, start, last=False):
        cols = pl.ds(pl.multiple_of(k * BK, BK), BK)

        @pl.loop(0, 2)
        def _(s):
            @pl.when(s == 1)
            def _():
                for f in range(2):
                    c_copy(0, k, f).wait_recv()

            @pl.loop(0, BK // 64)
            def _(q):
                rows = pl.ds(pl.multiple_of(q * 64, 64), 64)
                v = pool[pn.xb + s * nt + k, rows, :].astype(F32)
                v = (v - mi[s, rows, pl.ds(0, 1)]) * mi[s, rows, pl.ds(1, 1)]
                pool[pn.hb + s * nt + k, rows, :] = (v * gain[:, cols] + shift[:, cols]).astype(BF16)

            @pl.loop(0, nu)
            def _(u):
                out = mm(pool[pn.hb + s * nt + k], pool[pn.w1b + u * nt + k])
                if not start:
                    out = out + pre_v[s, :, at512(u)]
                pre_v[s, :, at512(u)] = out
                if last:
                    gelu_block(s, u, out)

    take(t, True)
    progress(1)
    pl.when(t >= 1)(lambda: take(t - 1, False))
    progress(2, (0,))
    pl.when(t + 1 < nt)(lambda: take(t + 1, False))
    progress(2, (1,))
    take(jnp.where(t >= 2, t - 2, t + 2), False)
    progress(3)
    for cp in tab_copies():
        cp.wait()

    @pl.when((t == 0) | (t == nt - 1))
    def _():
        take(nt - 1 - t, False, True)

    @pl.when((t > 0) & (t < nt - 1))
    def _():
        @pl.loop(0, 2 * nu)
        def _(i):
            s, u = i // nu, lax.rem(i, nu)
            gelu_block(s, u, pre_v[s, :, at512(u)])


    def biased(s, q):
        col = (2 * q + c if direct else q) * TW
        return pre_v[s, :, at256(q)] + b1[:, pl.ds(pl.multiple_of(col, TW), TW)]

    def tell(i):
        def signal(n, device):
            pl.semaphore_signal(credit.at[3 * i + n], inc=1, device_id=device, device_id_type=MESH)

        signal(0, place.pair())
        pl.when(t > 0)(lambda: signal(2, place.left()))
        pl.when(t < nt - 1)(lambda: signal(1, place.right()))

    def told(i):
        pl.semaphore_wait(credit.at[3 * i], 1)
        pl.when(t > 0)(lambda: pl.semaphore_wait(credit.at[3 * i + 1], 1))
        pl.when(t < nt - 1)(lambda: pl.semaphore_wait(credit.at[3 * i + 2], 1))

    tell(0)

    orders_ab = [list(range(pn.bits)), list(range(pn.bits))[::-1]]

    def piece(index, half, view, recv):
        return Piece(place, orders_ab[half], view, recv, s_p.at[index], r_p.at[index])

    per2 = BK // ub

    def view2(i, h):
        def view(j):
            return pool.at[
                pn.f2b + nu * i + j // per2,
                pl.ds(pl.multiple_of(lax.rem(j, per2) * ub, ub), ub),
                pl.ds(h * TW, TW),
            ]

        return view

    def view1(q, h):
        def view(j):
            r = 2 * j * rb + h * rb
            return pool.at[
                pn.f1b + nu * (r // BK) + q // 2,
                pl.ds(pl.multiple_of(lax.rem(r, BK), rb), rb),
                pl.ds((q % 2) * TW, TW),
            ]

        return view

    def view3(i, h):
        def view(j):
            r = 2 * j * rb + h * rb
            if i < 2:
                b, col = pn.f2b + r // BK, i * TW
            else:
                b, col = pn.f2b + nt + r // (2 * BK), pl.multiple_of(lax.rem(r // BK, 2) * TW, TW)
            return pool.at[b, pl.ds(pl.multiple_of(lax.rem(r, BK), rb), rb), pl.ds(col, TW)]

        return view

    def view_d(i):
        def view(j):
            return dg.at[pl.ds(pl.multiple_of(j * rd, rd), rd), pl.ds(i * BK, BK)]

        return view

    fc2_p = [[piece(2 * i + h, h, view2(i, h), rp.at[2 * i + h]) for h in range(2)] for i in range(nt)]
    fc1_p = [
        [piece(pn.n2 + 2 * q + h, h, view1(q, h), rp.at[pn.n2 + 2 * q + h]) for h in range(2)]
        for q in range(nq)
    ]
    qkv_p = [
        [piece(pn.n2 + pn.n1 + 2 * i + h, h, view3(i, h), rp.at[2 * i + h]) for h in range(2)]
        for i in range(3)
    ]
    den_p = [piece(pn.n2 + pn.n1 + pn.n3 + i, i % 2, view_d(i), dr.at[i]) for i in range(nt)]

    os_used = []

    def stage_out(value_to, dst):
        n = len(os_used)
        slot = n % ostage.shape[0]
        if n >= ostage.shape[0]:
            os_used[n - ostage.shape[0]].wait()
        value_to(ostage.at[slot])
        cp = pltpu.make_async_copy(ostage.at[slot, pl.ds(0, dst.shape[0]), :], dst, s_os.at[slot])
        cp.start()
        os_used.append(cp)

    def fin2(i):
        for h in range(2):
            p = fc2_p[i][h]
            p.wait(pn.bits - 1)

            def put(ref, p=p):
                p.final(ref)

            col = chunk(i) * BK + h * TW
            stage_out(put, fc2_out.at[:, pl.ds(pl.multiple_of(col, TW), TW)])

    def send_pair(slot):
        return remote(fs.at[slot], fr.at[slot], s_f.at[0, slot], s_f.at[1, slot], place.pair())

    def fin_pair(pieces, slot, dst):
        for h in range(2):
            pieces[h].wait(pn.bits - 1)

        def put(ref):
            for h in range(2):
                @pl.when(c == h)
                def _():
                    pieces[h].final(ref)

                @pl.when(c != h)
                def _():
                    pieces[h].final(fs.at[slot])

        stage_out(put, dst)
        send_pair(slot).start()

    def dst1(q, core):
        col = (2 * q + core) * TW if direct else core * pn.units + q * TW
        return fc1_out.at[:, pl.ds(pl.multiple_of(col, TW), TW)]

    def dst3(i, core):
        return qkv_out.at[i, :, pl.ds(pl.multiple_of(core * hw, hw), hw)]

    def fin1(q):
        fin_pair(fc1_p[q], q, dst1(q, c))

    def fin3(i):
        fin_pair(qkv_p[i], nq + i, dst3(i, c))

    def fin_d():
        for i in range(nt):
            p = den_p[i]
            p.wait(pn.bits - 1)
            for h in range(2):

                def put(ref, p=p, i=i, h=h):
                    half = pl.ds(h * TW, TW)
                    me = p.block(len(p.order), 0, True)
                    acc = dg[pl.ds(pl.multiple_of(me * rd, rd), rd), pl.ds(i * BK + h * TW, TW)].astype(F32)
                    for before in range(len(p.order)):
                        acc = acc + p.r[p.held(len(p.order), 0, before), :, half].astype(F32)
                    ref[pl.ds(0, rd), :] = acc

                col = chunk(i) * BK + h * TW
                stage_out(put, dense_out.at[:, pl.ds(pl.multiple_of(col, TW), TW)])

    def mids(pieces, i):
        for p in pieces:
            p.wait(i - 1)
            p.start(i)

    def mid(pieces):
        for i in range(1, pn.bits):
            mids(pieces, i)

    def fc2_chunk(i):
        k = chunk(i)
        for f in range(2):
            c_copy(1, k, f).wait_recv()
        for h in range(2):

            half = pl.ds(h * TW, TW)
            out = mm(buf[...], cat([pool[pn.cb + k, :, half], pool[pn.cb + nt + k, :, half]], 0)).astype(BF16)
            for u in range(nu):
                pool[pn.f2b + nu * i + u, :, half] = out[u * BK : (u + 1) * BK]
            fc2_p[i][h].start(0)

    done_steps = [nt - 1]

    def upto(step):
        while done_steps[0] < min(step, 2 * nt - 2):
            done_steps[0] += 1
            progress(done_steps[0])

    fc2_chunk(0)

    arrive("wq")
    lane = lax.broadcasted_iota(jnp.int32, (BK, TW), 1)
    low = lax.rem(lane, ROT) < ROT // 2

    def swap(v):
        return jnp.where(low, pltpu.roll(v, TW - ROT // 2, 1), pltpu.roll(v, ROT // 2, 1))

    def table(s, i):
        v = tab[s, :, pl.ds(i * LANES, LANES)]
        return jnp.concatenate([v, v], axis=1)

    @pl.loop(0, 2)
    def _(s):
        all_v = mm(cat([pool[pn.hb + s * nt + k] for k in range(nt)], 1), cat([wq_v[i] for i in range(3)], 1))
        for i in range(3):
            v = all_v[:, i * hw : (i + 1) * hw]
            cols = pl.ds(pl.multiple_of(c * hw, hw), hw)
            if i == 1:
                v = v + kbv[pl.ds(0, 1), :]
            else:
                v = v + qvb[pl.ds(i // 2, 1), cols]
            if i < 2:
                v = v * table(s, 0) + swap(v) * table(s, 1)
            qkv[i, s] = v.astype(BF16)

    upto(needed[1])
    fc2_chunk(1)
    z_sent(0)

    @pl.loop(0, 2 * nt)
    def _(i):
        for h in range(2):
            pool[pn.xb + i, :, pl.ds(h * TW, TW)] = pool[pn.hb + i, pl.ds(h * TW, TW), :].T

    mid(fc2_p[0])

    heads2 = [lane1 < HD, lane1 >= HD]
    score_scale = HD ** (-0.5)

    def only(v, h):
        return jnp.where(heads2[h], v, jnp.zeros_like(v))

    def bias_of(s, qt):
        nk = (qt + 1) * TW
        col = lax.broadcasted_iota(jnp.int32, (TW, nk), 1)
        row = lax.broadcasted_iota(jnp.int32, (TW, nk), 0) + qt * TW
        same = tab[s, pl.ds(qt * TW, TW), pl.ds(2 * LANES, 1)] == segr[s, pl.ds(0, 1), pl.ds(0, nk)]
        return jnp.where(same & (col <= row), 0.0, masked_score)

    def probs(qh, keys, bias):
        sc = mm(qh, keys, 1, 1) * score_scale + bias
        top = jnp.max(sc, axis=1, keepdims=True)
        ex = jnp.exp(sc - top)
        return ex * (1.0 / jnp.sum(ex, axis=1, keepdims=True))

    npair = hw // LANES

    def attention(s):
        @pl.loop(0, npair)
        def _(hp):
            cols = pl.ds(pl.multiple_of(hp * LANES, LANES), LANES)
            for qt in range(2):
                rows, kr = pl.ds(qt * TW, TW), pl.ds(0, (qt + 1) * TW)
                bias = bias_of(s, qt)
                out = []
                for h in range(2):
                    pb = probs(only(qkv[0, s, rows, cols], h), qkv[1, s, kr, cols], bias).astype(BF16)
                    out.append(mm(pb, qkv[2, s, kr, cols]))
                attn[s, rows, cols] = jnp.where(heads2[0], out[0], out[1]).astype(BF16)

    def attn_copy(s):
        return remote(attn.at[s], attn_p.at[1 - s], s_a.at[0, s], s_a.at[1, s], place.pair())

    attention(0)
    attn_copy(0).start()
    upto(needed[2])
    fc2_chunk(2)
    mid(fc2_p[1])
    attention(1)
    attn_copy(1).start()
    arrive("wd", "w2")

    class Line:
        def __init__(self, part, pr, rbase, sp, rp_, sl, rl):
            self.part, self.pr, self.rbase, self.sp, self.rp, self.sl, self.rl = part, pr, rbase, sp, rp_, sl, rl

        def pair(self, k):
            return remote(
                pool.at[self.part + nt + k], pool.at[self.pr + k], self.sp.at[k], self.rp.at[k], place.pair()
            )

        def copy(self, side, k, f, dev):
            slot = k if side == 0 else jnp.where(k == t - 1, nt, k)
            return remote(
                pool.at[self.part + k, at256(f), :],
                pool.at[self.rbase + slot, at256(f), :],
                self.sl.at[side, k, f],
                self.rl.at[slot, f],
                dev,
            )

        def got(self, slot, f):
            remote(
                pool.at[self.part, at256(f), :],
                pool.at[self.rbase + slot, at256(f), :],
                self.sl.at[0, 0, f],
                self.rl.at[slot, f],
                place.pair(),
            ).wait_recv()

        def each(self, side, step, do, which="all"):
            me = t if side == 0 else nt - 1 - t
            here = {"all": me <= step, "end": me == 0, "mid": (me > 0) & (me <= step)}[which]

            @pl.when(here & (me < nt - 1))
            def _():
                k = nt - 1 - step + me
                do(k if side == 0 else nt - 1 - k)

        def send(self, step, which):
            for side in range(2):

                def do(k, side=side):
                    for f in range(2):
                        if which == "mid":
                            self.got(k, f)

                        @pl.loop(0, TW // 64)
                        def _(q):
                            rows = pl.ds(pl.multiple_of(f * TW + q * 64, 64), 64)
                            v = pool[self.part + k, rows, :].astype(F32) + pool[self.pr + k, rows, :].astype(F32)
                            if which == "mid":
                                v = v + pool[self.rbase + k, rows, :].astype(F32)
                            pool[self.part + k, rows, :] = v.astype(BF16)

                        self.copy(side, k, f, z_dev(side)).start()

                self.each(side, step, do, which)

        def sent(self):
            for side in range(2):
                for step in range(nt - 1):
                    for f in range(2):
                        self.each(
                            side, step, lambda k, side=side, f=f: self.copy(side, k, f, place.pair()).wait_send()
                        )

        def finish(self, halves=(0, 1)):
            for f in halves:
                pl.when(t > 0)(lambda: self.got(t, f))
                pl.when(t < nt - 1)(lambda: self.got(nt, f))

        def value(self, rows):
            v = pool[self.part + t, rows, :].astype(F32) + pool[self.pr + t, rows, :].astype(F32)
            v = v + jnp.where(t > 0, pool[self.rbase + t, rows, :].astype(F32), 0.0)
            return v + jnp.where(t < nt - 1, pool[self.rbase + nt, rows, :].astype(F32), 0.0)

    line_o = Line(pn.hb, pn.w1b, pn.w1b + nt, s_oc, r_oc, s_ol, r_ol)
    line_h = Line(pn.hb, pn.w2b, pn.w2b + nt, s_hc, r_hc, s_hl, r_hl)
    def out_rows(s):
        @pl.loop(0, nt)
        def _(k):
            rhs = cat([wd_v[:, at512(k)]] + [pool[pn.w2b + u * nt + k] for u in range(nu)], 0)
            pool[pn.hb + s * nt + k] = mm(cat([attn[s], act[s]], 1), rhs).astype(BF16)

    out_rows(1)
    told(0)
    for k in range(nt):
        line_o.pair(k).start()

    for s in range(2):
        attn_copy(s).wait()
    for core in range(2):
        for s in range(2):
            mine = attn if core == 0 else attn_p
            v = jnp.where(live(s), mine[s], jnp.zeros((BK, hw), BF16))
            at_tmp[...] = v.T
            who = c if core == 0 else 1 - c
            for j in range(nch // 2):
                off = lax.rem((2 * j + c) * rd, hw)
                dst = (who * (nch // 2) + j) * rd
                dl[pl.ds(pl.multiple_of(dst, rd), rd), pl.ds(s * BK, BK)] = at_tmp[
                    pl.ds(pl.multiple_of(off, rd), rd), :
                ]

    def dense_chunk(i):
        k = chunk(i)
        out = mm(dl[...], cat([pool[pn.cb + k], pool[pn.cb + nt + k]], 0))
        dg[:, pl.ds(i * BK, BK)] = out.astype(BF16)
        den_p[i].start(0)

    mid(fc2_p[2])
    for i in range(nt - 1):
        dense_chunk(i)
    out_rows(0)
    upto(needed[3])
    for k in range(nt):
        line_o.pair(k).wait()
    @pl.loop(0, nt - 1)
    def _(step):
        line_o.send(step, "end")

    fc2_chunk(3)
    dense_chunk(3)

    def dpre_block(u):
        @pl.loop(0, 2)
        def _(s):
            v = mm(
                cat([pool[pn.cb + s * nt + k] for k in range(nt)], 1),
                cat([pool[pn.w2b + u * nt + k] for k in range(nt)], 1),
                1,
                1,
            )
            for h in range(2):
                q = 2 * u + h
                w = v[:, h * TW : (h + 1) * TW]
                w = jnp.where(live(s), w * gelu_slope(biased(s, q)), 0.0)
                buf[pl.ds(pl.multiple_of(s * BK, BK), BK), pl.ds(q * TW, TW)] = w.astype(BF16)
                fb[pl.ds(0, 1), pl.ds(q * TW, TW)] += jnp.sum(w, axis=0, keepdims=True)

    def fc1_block(u):
        @pl.loop(0, nt)
        def _(k):
            out = mm(cat([pool[pn.xb + k], pool[pn.xb + nt + k]], 1), buf[:, pl.ds(u * BK, BK)])
            pool[pn.f1b + nu * k + u] = out.astype(BF16)

        for q in (2 * u, 2 * u + 1):
            for p in fc1_p[q]:
                p.start(0)

    dpre_block(0)
    fc1_block(0)
    dpre_block(1)
    tell(1)
    fc1_block(1)
    line_o.send(1, "mid")
    mid(fc2_p[3])
    mid(den_p)

    def dcols(i):
        return pl.ds(i * hw, hw)

    @pl.loop(0, 2)
    def _(s):
        v = mm(cat([pool[pn.cb + s * nt + k] for k in range(nt)], 1), wd_v[...], 1, 1)
        v = jnp.where(live(s), v, 0.0)
        act[s, :, dcols(3)] = v.astype(BF16)

    ob[...] = jnp.broadcast_to(
        jnp.sum(jnp.where(live(0), pool[pn.cb + t].astype(F32), 0.0), axis=0, keepdims=True), ob.shape
    )
    z_sent(1)
    begin("w1r")
    fin2(0)
    fin2(1)
    @pl.loop(0, 2 * npair)
    def _(i):
        pl.when(i == npair)(lambda: line_o.send(2, "mid"))
        s, hp = i // npair, lax.rem(i, npair)
        cols = pl.ds(pl.multiple_of(hp * LANES, LANES), LANES)
        dq, dk, dv = [], [None, None], [None, None]
        for qt in range(2):
            rows, kr, nk = pl.ds(qt * TW, TW), pl.ds(0, (qt + 1) * TW), (qt + 1) * TW
            bias = bias_of(s, qt)
            da = act[s, rows, pl.ds(pl.multiple_of(3 * hw + hp * LANES, LANES), LANES)]
            prod = da.astype(F32) * attn[s, rows, cols].astype(F32)
            qs, ks, vs = qkv[0, s, rows, cols], qkv[1, s, kr, cols], qkv[2, s, kr, cols]
            got = []
            for h in range(2):
                pf = probs(only(qs, h), ks, bias)
                pb = pf.astype(BF16)
                delta = jnp.sum(only(prod, h), axis=1, keepdims=True)
                dp = mm(only(da, h), vs, 1, 1)
                ds = (pf * (dp - delta) * score_scale).astype(BF16)
                got.append((mm(ds, ks), mm(ds, qs, 0, 0), mm(pb, da, 0, 0)))
            pick = [jnp.where(heads2[0], a, b) for a, b in zip(*got)]
            dq.append(pick[0])
            for lst, v in ((dk, pick[1]), (dv, pick[2])):
                lst[0] = v[:TW] if lst[0] is None else lst[0] + v[:TW]
                if qt:
                    lst[1] = v[TW:]
        low1 = lax.rem(lane1, ROT) < ROT // 2
        for i3, parts in enumerate((dq, dk, dv)):
            for qt in range(2):
                rows = pl.ds(qt * TW, TW)
                v = parts[qt]
                if i3 < 2:
                    sw = jnp.where(
                        low1, pltpu.roll(v, LANES - ROT // 2, 1), pltpu.roll(v, ROT // 2, 1)
                    )
                    v = v * tab[s, rows, pl.ds(0, LANES)] - sw * tab[s, rows, pl.ds(LANES, LANES)]
                bias3[i3, pl.ds(0, 1), cols] += jnp.sum(v, axis=0, keepdims=True)
                act[s, rows, pl.ds(pl.multiple_of(i3 * hw + hp * LANES, LANES), LANES)] = v.astype(BF16)

    mid(fc1_p[0])
    mid(fc1_p[1])

    def dh_chunk(s, k):
        rhs = cat([wq_v[i, at512(k), :] for i in range(3)] + [pool[pn.cb + u * nt + k] for u in range(nu)], 1)
        lhs = cat([act[s, :, pl.ds(0, 3 * hw)], buf[pl.ds(s * BK, BK), :]], 1)
        pool[pn.hb + s * nt + k] = mm(lhs, rhs, 1, 1).astype(BF16)

    def step_of(tt, k):
        if k == tt:
            return nt
        return nt - 1 - k + tt if k > tt else k + nt - 1 - tt

    far = [sorted(range(nt), key=lambda k, tt=tt: (step_of(tt, k), k)) for tt in range(nt)]

    def far_chunk(i):
        k = 0
        for tt in range(nt):
            for n in range(nt):
                k = jnp.where((t == tt) & (i == n), far[tt][n], k)
        return k

    def qkv_blocks():
        @pl.loop(0, nt)
        def _(k):
            out = mm(
                cat([pool[pn.xb + k], pool[pn.xb + nt + k]], 1),
                cat([act[0, :, pl.ds(0, 3 * hw)], act[1, :, pl.ds(0, 3 * hw)]], 0),
            ).astype(BF16)
            pool[pn.f2b + k] = out[:, :BK]
            pool[pn.f2b + nt + k // 2, :, at256(lax.rem(k, 2))] = out[:, BK:]

        for i in range(3):
            for p in qkv_p[i]:
                p.start(0)

    told(1)
    arrive("w1r")
    @pl.loop(0, nt)
    def _(i):
        k = far_chunk(i)
        dh_chunk(1, k)
        line_h.pair(k).start()

    arrive("xo")
    line_o.finish()

    @pl.loop(0, BK // 64)
    def _(q):
        rows = pl.ds(pl.multiple_of(q * 64, 64), 64)
        ocol = pl.ds(pl.multiple_of(t * BK, BK), BK)
        v = pool[pn.xo, rows, :].astype(F32) + line_o.value(rows)
        v = v + (obias[pl.ds(0, 1), ocol] + obias[pl.ds(1, 1), ocol])
        block_out[rows, :] = v.astype(BF16)

    line_o.sent()
    @pl.loop(0, nt)
    def _(i):
        k = far_chunk(i)
        dh_chunk(0, k)
        line_h.pair(k).wait()
        pl.when(i < nt - 1)(lambda: line_h.send(i, "end"))

    fin2(2)
    fin2(3)
    for b in range(pn.bits):
        pl.semaphore_signal(credit.at[6 + b], inc=1, device_id=place.over(b), device_id_type=MESH)
    mid(fc1_p[2])
    for b in range(pn.bits):
        pl.semaphore_wait(credit.at[6 + b], 1)
    qkv_blocks()
    mid(fc1_p[3])
    line_h.send(1, "mid")
    fin1(0)
    mid(qkv_p[0])
    line_h.send(2, "mid")
    mid(qkv_p[1])
    mid(qkv_p[2])
    fin1(1)
    fin1(2)
    fin1(3)
    fin_d()
    fin3(0)

    gcol = pl.ds(pl.multiple_of(t * BK, BK), BK)

    def tail(rows):
        dh = line_h.value(rows)
        normed = (pool[pn.xo, rows, :].astype(F32) - mi[0, rows, pl.ds(0, 1)]) * mi[0, rows, pl.ds(1, 1)]
        return dh, normed, dh * gain[:, gcol]

    def s_copy(k, f):
        src = stt.at[:, pl.ds(f * TW, TW)]
        return remote(src, sr.at[t, :, pl.ds(f * TW, TW)], s_s.at[k, f], r_s.at[t, f], (d, lax.rem(t + k, nt)))

    def tail_one(f):
        line_h.finish((f,))

        @pl.loop(0, TW // 64)
        def _(q):
            rows = pl.ds(pl.multiple_of(f * TW + q * 64, 64), 64)
            dh, normed, scaled = tail(rows)
            s1 = jnp.sum(scaled, axis=1, keepdims=True)
            s2 = jnp.sum(scaled * normed, axis=1, keepdims=True)
            stc[rows, :] = jnp.where(first, s1, s2)
            ng[pl.ds(0, 1), :] += jnp.sum(dh * normed, axis=0, keepdims=True)
            ng[pl.ds(1, 1), :] += jnp.sum(dh, axis=0, keepdims=True)

        half = pl.ds(f * TW, TW)
        stt[:, half] = stc[half, :].T[:8]
        sr[t, :, half] = stt[:, half]
        for k in range(1, nt):
            s_copy(k, f).start()

    def tail_two(f):
        half = pl.ds(f * TW, TW)
        for k in range(1, nt):
            s_copy(k, f).wait_send()
            frm = lax.rem(t + k, nt)
            remote(
                stt.at[:, half], sr.at[frm, :, half], s_s.at[k, f], r_s.at[frm, f], place.pair()
            ).wait_recv()
        tot = sr[0, :, half]
        for k in range(1, nt):
            tot = tot + sr[k, :, half]
        stc[half, :] = jnp.concatenate([tot / pn.width, jnp.zeros((LANES - 8, TW), F32)], axis=0).T

        @pl.loop(0, TW // 64)
        def _(q):
            rows = pl.ds(pl.multiple_of(f * TW + q * 64, 64), 64)
            dh, normed, scaled = tail(rows)
            v = mi[0, rows, pl.ds(1, 1)] * (scaled - stc[rows, pl.ds(0, 1)] - normed * stc[rows, pl.ds(1, 1)])
            keep = tab[0, rows, pl.ds(2 * LANES, 1)] >= 0.0
            input_grad[rows, :] = v + jnp.where(keep, pool[pn.co, rows, :].astype(F32), 0.0)

    tail_one(0)
    fin3(1)
    tail_one(1)

    def v_copy(k):
        peer = lax.rem(d + k, nd)
        return remote(sv.at[peer], rv.at[d], s_v.at[k], r_v.at[d], (peer, t))

    cw, hwd = BK // nd, 2 * hw // nd
    sv[...] = jnp.zeros_like(sv)
    for dd in range(nd):
        mine = c == dd % 2
        sv[dd, pl.ds(0, 1), pl.ds(0, ub)] = jnp.where(mine, fb[pl.ds(0, 1), pl.ds((dd // 2) * ub, ub)], 0.0)
        sv[dd, pl.ds(1, 2), pl.ds(0, cw)] = ng[pl.ds(0, 2), pl.ds(dd * cw, cw)]
        sv[dd, pl.ds(3, 1), pl.ds(0, cw)] = ob[pl.ds(0, 1), pl.ds(dd * cw, cw)]
        here = c == (dd * hwd) // hw
        src = pl.ds((dd * hwd) % hw, hwd)
        sv[dd, pl.ds(4, 1), pl.ds(0, hwd)] = jnp.where(here, bias3[0, pl.ds(0, 1), src], 0.0)
        sv[dd, pl.ds(5, 1), pl.ds(0, hwd)] = jnp.where(here, bias3[2, pl.ds(0, 1), src], 0.0)
        for core in range(2):
            sv[dd, pl.ds(6 + core, 1), :] = jnp.where(c == core, bias3[1, pl.ds(0, 1), :], 0.0)
    for k in range(1, nd):
        v_copy(k).start()
    rv[d] = sv[d]
    tail_two(0)
    fin3(2)
    for slot in range(nq + 3):
        send_pair(slot).wait()

        def put(ref, slot=slot):
            ref[pl.ds(0, rb), :] = fr[slot].astype(F32)

        stage_out(put, dst1(slot, 1 - c) if slot < nq else dst3(slot - nq, 1 - c))
    tail_two(1)
    line_h.sent()
    for k in range(1, nd):
        v_copy(k).wait_send()
        frm = lax.rem(d + k, nd)
        remote(sv.at[0], rv.at[frm], s_v.at[k], r_v.at[frm], place.pair()).wait_recv()
    res = rv[0]
    for k in range(1, nd):
        res = res + rv[k]
    fc1b_out[...] = res[0:1, :ub]
    norm_out[...] = res[1:3, :cw]
    outb_out[...] = jnp.concatenate([res[3:4, :cw], res[3:4, :cw]], axis=0)
    qvb_out[...] = res[4:6, :hwd]
    rk = ROT // nd
    turned = pltpu.roll(res, lax.rem(TW - d * rk, TW), 1)
    for core in range(2):
        for h in range(pn.heads):
            stc[pl.ds(core * pn.heads + h, 1), pl.ds(0, rk)] = turned[6 + core : 7 + core, h * HD : h * HD + rk]
    keyb_out[...] = stc[pl.ds(0, LANES), :].T[:rk, : 2 * pn.heads]
    for cp in os_used[-ostage.shape[0] :]:
        cp.wait()

def copy_kernel(n, *refs):
    src, dst, hold, sem = refs[:n], refs[n : 2 * n], refs[2 * n : 3 * n], refs[3 * n]

    def go(i, out):
        a, b = (hold[i], dst[i]) if out else (src[i], hold[i])
        return pltpu.make_async_copy(a, b, sem.at[int(out), i])

    for i in range(n):
        go(i, False).start()
    for i in range(n):
        go(i, False).wait()
        go(i, True).start()
    for i in range(n):
        go(i, True).wait()


def copied(arrays):
    n = len(arrays)
    shapes = [jax.ShapeDtypeStruct(a.shape, a.dtype) for a in arrays]
    return pl.pallas_call(
        functools.partial(copy_kernel, n),
        out_shape=shapes,
        in_specs=[pl.BlockSpec(memory_space=pl.ANY)] * n,
        out_specs=[pl.BlockSpec(memory_space=pl.ANY)] * n,
        scratch_shapes=[pltpu.VMEM(a.shape, a.dtype) for a in arrays] + [pltpu.SemaphoreType.DMA((2, n))],
        compiler_params=pltpu.CompilerParams(vmem_limit_bytes=VMEM_BYTES),
        name="results",
    )(*arrays)


def per_device(
    hidden_in,
    cotangent,
    segment_ids,
    positions,
    norm_gain,
    norm_shift,
    qkv_weight,
    qv_bias,
    key_bias,
    dense_weight,
    fc1_weight,
    fc1_bias,
    fc2_weight,
    out_bias,
):
    nd, nt = lax.axis_size("dp"), lax.axis_size("tensor")
    c = lax.rem(lax.axis_index("dp"), 2)
    nch = nd // 2
    rows, wl = hidden_in.shape
    width = wl * nt
    heads = key_bias.shape[0] // 2
    units = fc1_weight.shape[1] // 2
    ub = units // nch
    pn = Plan(nd, nt, units, heads, ub)
    hw, rb, rd, nq = pn.hw, pn.rb, pn.rd, units // TW
    assert rows == BK and wl == BK and nt == 4 and nq == 4 and hw == TW and rb == ub
    direct = ub == TW

    freq = 10000.0 ** (-(np.arange(LANES) % (ROT // 2)) * (2.0 / ROT))
    freq = jnp.asarray(freq.astype(np.float32)[None, :])

    def pick(w, axis):
        shape = w.shape
        w = w.reshape(*shape[:axis], nch, 2, ub, *shape[axis + 1 :])
        w = lax.dynamic_index_in_dim(w, c, axis + 1, keepdims=False)
        return w.reshape(*shape[:axis], units, *shape[axis + 1 :])

    w1, w2, b1 = fc1_weight, fc2_weight, fc1_bias
    if not direct:
        w1, w2, b1 = pick(w1, 1), pick(w2, 0), pick(b1, 0)
    w1 = w1.reshape(nt, BK, w1.shape[1])
    wq = qkv_weight.transpose(1, 0, 2)
    b1 = b1.reshape(1, -1)

    vm = pl.BlockSpec(memory_space=pltpu.VMEM)
    anyw = pl.BlockSpec(memory_space=pl.ANY)
    shapes = [
        ((rows, wl), BF16, vm),
        ((rows, wl), F32, vm),
        ((2, wl // nd), F32, vm),
        ((3, rb, 2 * hw), F32, anyw),
        ((2, 2 * hw // nd), F32, vm),
        ((ROT // nd, 2 * heads), F32, vm),
        ((rd, width), F32, anyw),
        ((rb, 2 * units), F32, anyw),
        ((1, ub), F32, vm),
        ((ub, width), F32, anyw),
        ((2, wl // nd), F32, vm),
    ]
    dma = pltpu.SemaphoreType.DMA
    nos = 4
    scratch = [
        pltpu.VMEM((pn.blocks, BK, BK), BF16),
        pltpu.VMEM((3, width, hw), BF16),
        pltpu.VMEM((hw, width), BF16),
        pltpu.VMEM((2, rows, 3 * LANES), F32),
        pltpu.VMEM((2, 8, rows), F32),
        pltpu.VMEM((2, rows, units), BF16),
        pltpu.VMEM((units, 2 * rows), BF16),
        pltpu.VMEM((2, rows, units), F32),
        pltpu.VMEM((3, 2, rows, hw), BF16),
        pltpu.VMEM((2, rows, hw), BF16),
        pltpu.VMEM((2, rows, hw), BF16),
        pltpu.VMEM((nch * rd, 2 * rows), BF16),
        pltpu.VMEM((hw, rows), BF16),
        pltpu.VMEM((nch * rd, width), BF16),
        pltpu.VMEM((nt, nch - 1, rd, BK), BF16),
        pltpu.VMEM((pn.n2 + pn.n1, nch - 1, rb, TW), BF16),
        pltpu.VMEM((nq + 3, rb, TW), BF16),
        pltpu.VMEM((nq + 3, rb, TW), BF16),
        pltpu.VMEM((nos, max(rb, rd), TW), F32),
        pltpu.VMEM((2, rows, LANES), F32),
        pltpu.VMEM((3, 8, hw), F32),
        pltpu.VMEM((8, units), F32),
        pltpu.VMEM((8, wl), F32),
        pltpu.VMEM((8, wl), F32),
        pltpu.VMEM((nd, 8, TW), F32),
        pltpu.VMEM((nd, 8, TW), F32),
        pltpu.VMEM((rows, LANES), F32),
        pltpu.VMEM((8, rows), F32),
        pltpu.VMEM((nt, 8, rows), F32),
        pltpu.VMEM((2, nt, 8, rows), F32),
        pltpu.VMEM((8, hw), F32),
        dma((10 + nq * (2 + nt),)),
        dma((2, 2, nt, 2)),
        dma((2, nt, 2)),
        dma((2, nt, 2)),
        dma((2, nt, 2)),
        dma((4,)),
        dma((pn.pieces, nch - 1)),
        dma((pn.pieces, nch - 1)),
        dma((2,)),
        dma((2,)),
        dma((2, nq + 3)),
        dma((nos,)),
        dma((2, 2)),
        dma((nt,)),
        dma((nt,)),
        dma((2, nt, 2)),
        dma((nt + 1, 2)),
        dma((nt,)),
        dma((nt,)),
        dma((2, nt, 2)),
        dma((nt + 1, 2)),
        dma((nd,)),
        dma((nd,)),
        dma((nt, 2)),
        dma((nt, 2)),
        dma((2, nt)),
        dma((2, nt)),
        pltpu.SemaphoreType.REGULAR((6 + pn.bits,)),
    ]
    res = pl.pallas_call(
        functools.partial(block_kernel, pn, direct),
        out_shape=[jax.ShapeDtypeStruct(s, dt) for s, dt, _ in shapes],
        in_specs=[anyw, anyw, vm, vm, vm, vm, vm, anyw, anyw, anyw, anyw, vm, vm, vm, vm],
        out_specs=[sp for _, _, sp in shapes],
        scratch_shapes=scratch,
        compiler_params=pltpu.CompilerParams(
            collective_id=0, has_side_effects=True, vmem_limit_bytes=VMEM_BYTES
        ),
        name="block",
    )(
        hidden_in, cotangent, segment_ids.reshape(1, rows), positions.reshape(1, rows), freq, norm_gain.reshape(1, width), norm_shift.reshape(1, width),
        w1, w2, wq, dense_weight, b1, qv_bias, key_bias, out_bias,
    )
    res = list(copied(res))
    res[3] = res[3].transpose(1, 0, 2)
    res[5] = res[5].T
    if not direct:
        res[7] = res[7].reshape(rb, 2, nch, ub).transpose(0, 2, 1, 3).reshape(rb, 2 * units)
    res[8] = res[8].reshape(ub)
    return tuple(res)


def solution(mesh):
    placed = (
        P("dp", "tensor"),
        P("dp", "tensor"),
        P("dp"),
        P("dp"),
        P(),
        P(),
        P(None, None, "tensor"),
        P(None, "tensor"),
        P("tensor", None),
        P("tensor", None),
        P(None, "tensor"),
        P("tensor"),
        P("tensor", None),
        P(),
    )
    return jax.shard_map(
        per_device,
        mesh=mesh,
        in_specs=placed,
        out_specs=(
            P("dp", "tensor"),
            P("dp", "tensor"),
            P(None, ("tensor", "dp")),
            P("dp", None, "tensor"),
            P(None, ("tensor", "dp")),
            P("tensor", "dp"),
            P(("tensor", "dp"), None),
            P("dp", "tensor"),
            P(("tensor", "dp")),
            P(("tensor", "dp"), None),
            P(None, ("tensor", "dp")),
        ),
        check_vma=False,
    )
```

profile of v0, /device:TPU:0, one launch (start us, length us, event | category | flops | bytes accessed | tf_op | source)
XLA Modules:
  0.0 178.5 jit_solution(8124610868868494078)
XLA Ops:
  0.6 171.3 %block.1 = (bf16[512,512]{1,0:T(8,128)(2,1)}, f32[512,512]{1,0:T(8,128)}, f32[2,64]{1,0:T(2,128)}, f32[3,256,512]{2,1,0:T(8,128)}, f32[2,64]{1,0:T(2,128)}, /*in...) custom-call(bf16[512,512]{1,0:T(8,128)(2,1)} %refs_0_.1, ...), custom_call_target="tpu_custom_call" | custom-call | tf_op jit(solution)/shard_map/block/pallas_call | solution.py:1316
  172.0 6.3 %results.1 = (bf16[512,512]{1,0:T(8,128)(2,1)}, f32[512,512]{1,0:T(8,128)}, f32[2,64]{1,0:T(2,128)}, f32[3,256,512]{2,1,0:T(8,128)}, f32[2,64]{1,0:T(2,128)}, /*...) custom-call(bf16[512,512]{1,0:T(8,128)(2,1)} %get-tuple-element.33.r, ...), custom_call_target="tpu_custom_call" | custom-call | tf_op jit(solution)/shard_map/results/pallas_call | solution.py:1182
where the time goes:
time: 179 us; the launch traced here: 178 us
  Pallas kernels  178 us (99%)
    pallas_call x1, Pallas kernels, per_device(): pl.pallas_call(functools.partial(block_kernel, pn, direct), out_shape=[ja...  171 us
    pallas_call x1, Pallas kernels, copied(): pl.pallas_call(functools.partial(copy_kernel, n), out_shape=shapes, in_sp...  6.28 us

commit v1 on v0

--- a/solution.py
+++ b/solution.py
@@ -1,4 +1,5 @@
 import functools
+import math
 
 import jax
 import jax.numpy as jnp
@@ -214,9 +215,9 @@
     (
         x_in, c_in, seg_in, pos_in, freq, gain, shift, w1, w2, wq, wd, b1, qvb, kb, obias,
         block_out, input_grad, norm_out, qkv_out, qvb_out, keyb_out, dense_out, fc1_out, fc1b_out,
-        fc2_out, outb_out,
+        fc2_out, outb_out, other_out,
         pool, wq_v, wd_v, tab, segr, act, buf, pre_v, qkv, attn, attn_p, dl, at_tmp, dg, dr, rp, fs, fr,
-        ostage, mi, bias3, fb, ob, ng, sv, rv, stc, stt, sr, st, kbv,
+        ostage, mi, bias3, fb, ob, ng, sv, rv, stc, stt, sr, st, kbv, stk,
         s_load, s_z, r_z, s_c, r_c, s_tab, s_p, r_p, s_d, r_d, s_f, s_os, s_a, s_oc, r_oc, s_ol, r_ol,
         s_hc, r_hc, s_hl, r_hl, s_v, r_v, s_s, r_s, s_st, r_st, credit,
     ) = refs
@@ -264,7 +265,7 @@
             for cp in loads[name]:
                 cp.wait()
 
-    begin("x", "c", "w1", "wq", "wd", "w2", "xo")
+    begin("x")
     greet(place)
     arrive("x")
 
@@ -278,7 +279,11 @@
         v = v - m
         stc[rows, :] = jnp.where(first, m, jnp.sum(v * v, axis=1, keepdims=True))
 
-    stt[...] = stc[...].T[:8]
+    for j in range(4):
+        turned = stc[pl.ds(j * LANES, LANES), :].T
+        stk[pl.ds(j, 1), :] = turned[0:1]
+        stk[pl.ds(4 + j, 1), :] = turned[1:2]
+
     greeted(place)
 
     def blk(a, s, k, f):
@@ -383,7 +388,7 @@
     def st_copy(s, k):
         peer = lax.rem(t + k, nt)
         dev = (d, peer) if s == 0 else (place.pair()[0], peer)
-        return remote(stt, st.at[s, t], s_st.at[s, k], r_st.at[s, t], dev)
+        return remote(stk, st.at[s, t], s_st.at[s, k], r_st.at[s, t], dev)
 
     for k in range(nt):
         for s in range(2):
@@ -392,7 +397,8 @@
     progress(0)
     for f in range(2):
         own_c(0, f).start()
-    st[0, t] = stt[...]
+    st[0, t] = stk[...]
+    begin("w1", "c")
 
     def column(row):
         return jnp.broadcast_to(row.astype(F32), (LANES, BK)).T
@@ -422,16 +428,17 @@
             if k or s:
                 frm = lax.rem(t + k, nt)
                 st_copy(s, k).wait_send()
-                remote(stt, st.at[s, frm], s_st.at[s, k], r_st.at[s, frm], place.pair()).wait_recv()
+                remote(stk, st.at[s, frm], s_st.at[s, k], r_st.at[s, frm], place.pair()).wait_recv()
     for s in range(2):
-        mean = sum(st[s, k, pl.ds(0, 1), :] for k in range(nt)) / nt
+        mean = sum(st[s, k, pl.ds(0, 4), :] for k in range(nt)) / nt
         dev = 0.0
         for k in range(nt):
-            off = st[s, k, pl.ds(0, 1), :] - mean
-            dev = dev + st[s, k, pl.ds(1, 1), :] + BK * off * off
+            off = st[s, k, pl.ds(0, 4), :] - mean
+            dev = dev + st[s, k, pl.ds(4, 4), :] + BK * off * off
         inv = lax.rsqrt(dev / pn.width + norm_epsilon)
-        both = jnp.concatenate([mean, inv, jnp.zeros((LANES - 2, BK), F32)], axis=0)
-        mi[s] = both.T
+        for j in range(4):
+            both = cat([mean[j : j + 1], inv[j : j + 1], jnp.zeros((LANES - 2, LANES), F32)], 0)
+            mi[s, pl.ds(j * LANES, LANES), :] = both.T
     arrive("w1")
 
     def live(s):
@@ -475,6 +482,7 @@
                     gelu_block(s, u, out)
 
     take(t, True)
+    begin("wq", "wd", "w2", "xo")
     progress(1)
     pl.when(t >= 1)(lambda: take(t - 1, False))
     progress(2, (0,))
@@ -615,18 +623,17 @@
         stage_out(put, dst)
         send_pair(slot).start()
 
-    def dst1(q, core):
-        col = (2 * q + core) * TW if direct else core * pn.units + q * TW
-        return fc1_out.at[:, pl.ds(pl.multiple_of(col, TW), TW)]
-
-    def dst3(i, core):
-        return qkv_out.at[i, :, pl.ds(pl.multiple_of(core * hw, hw), hw)]
+    def dst1(q):
+        return fc1_out.at[:, pl.ds(q * TW, TW)]
+
+    def dst3(i):
+        return qkv_out.at[i]
 
     def fin1(q):
-        fin_pair(fc1_p[q], q, dst1(q, c))
+        fin_pair(fc1_p[q], q, dst1(q))
 
     def fin3(i):
-        fin_pair(qkv_p[i], nq + i, dst3(i, c))
+        fin_pair(qkv_p[i], nq + i, dst3(i))
 
     def fin_d():
         for i in range(nt):
@@ -709,6 +716,7 @@
         for h in range(2):
             pool[pn.xb + i, :, pl.ds(h * TW, TW)] = pool[pn.hb + i, pl.ds(h * TW, TW), :].T
 
+
     mid(fc2_p[0])
 
     heads2 = [lane1 < HD, lane1 >= HD]
@@ -787,7 +795,7 @@
 
         def each(self, side, step, do, which="all"):
             me = t if side == 0 else nt - 1 - t
-            here = {"all": me <= step, "end": me == 0, "mid": (me > 0) & (me <= step)}[which]
+            here = {"all": me <= step, "end": me == 0, "far": (me > 1) & (me <= step), "near": me == 1}[which]
 
             @pl.when(here & (me < nt - 1))
             def _():
@@ -799,14 +807,14 @@
 
                 def do(k, side=side):
                     for f in range(2):
-                        if which == "mid":
+                        if which != "end":
                             self.got(k, f)
 
                         @pl.loop(0, TW // 64)
                         def _(q):
                             rows = pl.ds(pl.multiple_of(f * TW + q * 64, 64), 64)
                             v = pool[self.part + k, rows, :].astype(F32) + pool[self.pr + k, rows, :].astype(F32)
-                            if which == "mid":
+                            if which != "end":
                                 v = v + pool[self.rbase + k, rows, :].astype(F32)
                             pool[self.part + k, rows, :] = v.astype(BF16)
 
@@ -911,7 +919,7 @@
     dpre_block(1)
     tell(1)
     fc1_block(1)
-    line_o.send(1, "mid")
+    line_o.send(1, "near")
     mid(fc2_p[3])
     mid(den_p)
 
@@ -933,7 +941,7 @@
     fin2(1)
     @pl.loop(0, 2 * npair)
     def _(i):
-        pl.when(i == npair)(lambda: line_o.send(2, "mid"))
+        pl.when(i == npair)(lambda: line_o.send(2, "far"))
         s, hp = i // npair, lax.rem(i, npair)
         cols = pl.ds(pl.multiple_of(hp * LANES, LANES), LANES)
         dq, dk, dv = [], [None, None], [None, None]
@@ -970,6 +978,7 @@
                 bias3[i3, pl.ds(0, 1), cols] += jnp.sum(v, axis=0, keepdims=True)
                 act[s, rows, pl.ds(pl.multiple_of(i3 * hw + hp * LANES, LANES), LANES)] = v.astype(BF16)
 
+    line_o.send(2, "near")
     mid(fc1_p[0])
     mid(fc1_p[1])
 
@@ -1023,7 +1032,12 @@
         ocol = pl.ds(pl.multiple_of(t * BK, BK), BK)
         v = pool[pn.xo, rows, :].astype(F32) + line_o.value(rows)
         v = v + (obias[pl.ds(0, 1), ocol] + obias[pl.ds(1, 1), ocol])
-        block_out[rows, :] = v.astype(BF16)
+        pool[pn.w1b + t, rows, :] = v.astype(BF16)
+
+    def out_copy():
+        return pltpu.make_async_copy(pool.at[pn.w1b + t], block_out, s_load.at[2])
+
+    out_copy().start()
 
     line_o.sent()
     @pl.loop(0, nt)
@@ -1042,17 +1056,15 @@
         pl.semaphore_wait(credit.at[6 + b], 1)
     qkv_blocks()
     mid(fc1_p[3])
-    line_h.send(1, "mid")
+    line_h.send(1, "near")
     fin1(0)
     mid(qkv_p[0])
-    line_h.send(2, "mid")
+    line_h.send(2, "far")
     mid(qkv_p[1])
+    line_h.send(2, "near")
     mid(qkv_p[2])
     fin1(1)
     fin1(2)
-    fin1(3)
-    fin_d()
-    fin3(0)
 
     gcol = pl.ds(pl.multiple_of(t * BK, BK), BK)
 
@@ -1097,16 +1109,32 @@
             tot = tot + sr[k, :, half]
         stc[half, :] = jnp.concatenate([tot / pn.width, jnp.zeros((LANES - 8, TW), F32)], axis=0).T
 
-        @pl.loop(0, TW // 64)
-        def _(q):
-            rows = pl.ds(pl.multiple_of(f * TW + q * 64, 64), 64)
-            dh, normed, scaled = tail(rows)
-            v = mi[0, rows, pl.ds(1, 1)] * (scaled - stc[rows, pl.ds(0, 1)] - normed * stc[rows, pl.ds(1, 1)])
-            keep = tab[0, rows, pl.ds(2 * LANES, 1)] >= 0.0
-            input_grad[rows, :] = v + jnp.where(keep, pool[pn.co, rows, :].astype(F32), 0.0)
+        for h in range(2):
+
+            def put(ref, h=h):
+                @pl.loop(0, TW // 64)
+                def _(q):
+                    rows = pl.ds(pl.multiple_of(f * TW + q * 64, 64), 64)
+                    part = slice(h * TW, (h + 1) * TW)
+                    _, normed, scaled = (v[:, part] for v in tail(rows))
+                    v = scaled - stc[rows, pl.ds(0, 1)] - normed * stc[rows, pl.ds(1, 1)]
+                    keep = tab[0, rows, pl.ds(2 * LANES, 1)] >= 0.0
+                    own = pool[pn.co, rows, pl.ds(h * TW, TW)].astype(F32)
+                    ref[pl.ds(pl.multiple_of(q * 64, 64), 64), :] = v * mi[0, rows, pl.ds(1, 1)] + jnp.where(
+                        keep, own, 0.0
+                    )
+
+            stage_out(put, input_grad.at[pl.ds(f * TW, TW), pl.ds(h * TW, TW)])
+
+    def pass_on(slot):
+        return pltpu.make_async_copy(fr.at[slot], other_out.at[slot], s_f.at[2, slot])
+
+    def pass_all(lo, hi):
+        for slot in range(lo, hi):
+            send_pair(slot).wait()
+            pass_on(slot).start()
 
     tail_one(0)
-    fin3(1)
     tail_one(1)
 
     def v_copy(k):
@@ -1129,16 +1157,15 @@
     for k in range(1, nd):
         v_copy(k).start()
     rv[d] = sv[d]
+    fin1(3)
+    fin_d()
+    pass_all(0, nq)
+    fin3(0)
+    fin3(1)
     tail_two(0)
     fin3(2)
-    for slot in range(nq + 3):
-        send_pair(slot).wait()
-
-        def put(ref, slot=slot):
-            ref[pl.ds(0, rb), :] = fr[slot].astype(F32)
-
-        stage_out(put, dst1(slot, 1 - c) if slot < nq else dst3(slot - nq, 1 - c))
     tail_two(1)
+    pass_all(nq, nq + 3)
     line_h.sent()
     for k in range(1, nd):
         v_copy(k).wait_send()
@@ -1157,34 +1184,73 @@
         for h in range(pn.heads):
             stc[pl.ds(core * pn.heads + h, 1), pl.ds(0, rk)] = turned[6 + core : 7 + core, h * HD : h * HD + rk]
     keyb_out[...] = stc[pl.ds(0, LANES), :].T[:rk, : 2 * pn.heads]
+    for slot in range(nq + 3):
+        pass_on(slot).wait()
+    out_copy().wait()
     for cp in os_used[-ostage.shape[0] :]:
         cp.wait()
 
-def copy_kernel(n, *refs):
-    src, dst, hold, sem = refs[:n], refs[n : 2 * n], refs[2 * n : 3 * n], refs[3 * n]
-
-    def go(i, out):
-        a, b = (hold[i], dst[i]) if out else (src[i], hold[i])
-        return pltpu.make_async_copy(a, b, sem.at[int(out), i])
-
-    for i in range(n):
-        go(i, False).start()
-    for i in range(n):
-        go(i, False).wait()
-        go(i, True).start()
-    for i in range(n):
-        go(i, True).wait()
-
-
-def copied(arrays):
-    n = len(arrays)
-    shapes = [jax.ShapeDtypeStruct(a.shape, a.dtype) for a in arrays]
+def results_kernel(nq, direct, *refs):
+    n = len(refs) // 3 - 1
+    src, dst, hold = refs[: n + 1], refs[n + 1 : 2 * n + 1], refs[2 * n + 1 : 3 * n + 2]
+    wide, sem, sem_w = refs[3 * n + 2 :]
+    c = lax.rem(lax.axis_index("dp"), 2)
+    order = sorted(range(n + 1), key=lambda i: -math.prod(src[i].shape))
+    order = [n] + [i for i in order if i != n]
+
+    def get(i):
+        return pltpu.make_async_copy(src[i], hold[i], sem.at[0, i])
+
+    def parts(i):
+        if i not in (3, 7):
+            return [(hold[i], dst[i])]
+        m = 3 if i == 3 else nq
+        out = []
+        for k in range(m):
+            if i == 3:
+                own, at = hold[3].at[k], lambda core, k=k: dst[3].at[k, :, at256(core)]
+            else:
+                own = hold[7].at[:, pl.ds(k * TW, TW)]
+                at = lambda core, k=k: dst[7].at[:, at256(2 * k + core if direct else core * nq + k)]
+            out += [(own, at(c)), (wide.at[nq + k if i == 3 else k], at(1 - c))]
+        return out
+
+    count = [0]
+
+    def put(i):
+        for a, b in parts(i):
+            cp = pltpu.make_async_copy(a, b, sem_w.at[count[0]])
+            count[0] += 1
+            cp.start()
+            sent.append(cp)
+
+    sent = []
+    for i in order:
+        get(i).start()
+    for i in order:
+        get(i).wait()
+        if i == n:
+            wide[...] = hold[n][...].astype(F32)
+        else:
+            put(i)
+    for cp in sent:
+        cp.wait()
+
+
+def results(arrays, nq, direct, shapes):
+    n = len(shapes)
+    anyw = pl.BlockSpec(memory_space=pl.ANY)
     return pl.pallas_call(
-        functools.partial(copy_kernel, n),
-        out_shape=shapes,
-        in_specs=[pl.BlockSpec(memory_space=pl.ANY)] * n,
-        out_specs=[pl.BlockSpec(memory_space=pl.ANY)] * n,
-        scratch_shapes=[pltpu.VMEM(a.shape, a.dtype) for a in arrays] + [pltpu.SemaphoreType.DMA((2, n))],
+        functools.partial(results_kernel, nq, direct),
+        out_shape=[jax.ShapeDtypeStruct(s, a.dtype) for s, a in zip(shapes, arrays)],
+        in_specs=[anyw] * (n + 1),
+        out_specs=[anyw] * n,
+        scratch_shapes=[pltpu.VMEM(a.shape, a.dtype) for a in arrays]
+        + [
+            pltpu.VMEM(arrays[n].shape, F32),
+            pltpu.SemaphoreType.DMA((1, n + 1)),
+            pltpu.SemaphoreType.DMA((n - 2 + 2 * (nq + 3),)),
+        ],
         compiler_params=pltpu.CompilerParams(vmem_limit_bytes=VMEM_BYTES),
         name="results",
     )(*arrays)
@@ -1238,17 +1304,18 @@
     vm = pl.BlockSpec(memory_space=pltpu.VMEM)
     anyw = pl.BlockSpec(memory_space=pl.ANY)
     shapes = [
-        ((rows, wl), BF16, vm),
-        ((rows, wl), F32, vm),
+        ((rows, wl), BF16, anyw),
+        ((rows, wl), F32, anyw),
         ((2, wl // nd), F32, vm),
-        ((3, rb, 2 * hw), F32, anyw),
+        ((3, rb, hw), F32, anyw),
         ((2, 2 * hw // nd), F32, vm),
         ((ROT // nd, 2 * heads), F32, vm),
         ((rd, width), F32, anyw),
-        ((rb, 2 * units), F32, anyw),
+        ((rb, units), F32, anyw),
         ((1, ub), F32, vm),
         ((ub, width), F32, anyw),
         ((2, wl // nd), F32, vm),
+        ((nq + 3, rb, TW), BF16, anyw),
     ]
     dma = pltpu.SemaphoreType.DMA
     nos = 4
@@ -1271,7 +1338,7 @@
         pltpu.VMEM((pn.n2 + pn.n1, nch - 1, rb, TW), BF16),
         pltpu.VMEM((nq + 3, rb, TW), BF16),
         pltpu.VMEM((nq + 3, rb, TW), BF16),
-        pltpu.VMEM((nos, max(rb, rd), TW), F32),
+        pltpu.VMEM((nos, TW, TW), F32),
         pltpu.VMEM((2, rows, LANES), F32),
         pltpu.VMEM((3, 8, hw), F32),
         pltpu.VMEM((8, units), F32),
@@ -1282,8 +1349,9 @@
         pltpu.VMEM((rows, LANES), F32),
         pltpu.VMEM((8, rows), F32),
         pltpu.VMEM((nt, 8, rows), F32),
-        pltpu.VMEM((2, nt, 8, rows), F32),
+        pltpu.VMEM((2, nt, 8, LANES), F32),
         pltpu.VMEM((8, hw), F32),
+        pltpu.VMEM((8, LANES), F32),
         dma((10 + nq * (2 + nt),)),
         dma((2, 2, nt, 2)),
         dma((2, nt, 2)),
@@ -1294,7 +1362,7 @@
         dma((pn.pieces, nch - 1)),
         dma((2,)),
         dma((2,)),
-        dma((2, nq + 3)),
+        dma((3, nq + 3)),
         dma((nos,)),
         dma((2, 2)),
         dma((nt,)),
@@ -1327,7 +1395,9 @@
         hidden_in, cotangent, segment_ids.reshape(1, rows), positions.reshape(1, rows), freq, norm_gain.reshape(1, width), norm_shift.reshape(1, width),
         w1, w2, wq, dense_weight, b1, qv_bias, key_bias, out_bias,
     )
-    res = list(copied(res))
+    whole = [s for s, _, _ in shapes[:-1]]
+    whole[3], whole[7] = (3, rb, 2 * hw), (rb, 2 * units)
+    res = list(results(res, nq, direct, whole))
     res[3] = res[3].transpose(1, 0, 2)
     res[5] = res[5].T
     if not direct:

time: 179 us -> 174 us (0.972)
  Pallas kernels: 178 us -> 173 us
    pallas_call x1, Pallas kernels: 171 us -> 168 us  [per_device(): pl.pallas_call(functools.partial(block_kernel, pn, direct), out_shape=[ja...]
where the time goes in v1:
time: 174 us
  Pallas kernels  173 us (99%)
    pallas_call x1, Pallas kernels, per_device(): pl.pallas_call(functools.partial(block_kernel, pn, direct), out_shape=[ja...  168 us
    pallas_call x1, Pallas kernels, results(): pl.pallas_call(functools.partial(results_kernel, nq, direct), out_shape=[...  5.32 us

profile of v1, /device:TPU:0, one launch (start us, length us, event | category | flops | bytes accessed | tf_op | source)
XLA Modules:
  0.0 174.0 jit_solution(3789994720998901823)
XLA Ops:
  0.6 167.9 %block.1 = (bf16[512,512]{1,0:T(8,128)(2,1)}, f32[512,512]{1,0:T(8,128)}, f32[2,64]{1,0:T(2,128)}, f32[3,256,256]{2,1,0:T(8,128)}, f32[2,64]{1,0:T(2,128)}, /*in...) custom-call(bf16[512,512]{1,0:T(8,128)(2,1)} %refs_0_.1, ...), custom_call_target="tpu_custom_call" | custom-call | tf_op jit(solution)/shard_map/block/pallas_call | solution.py:1384
  168.5 5.3 %results.1 = (bf16[512,512]{1,0:T(8,128)(2,1)}, f32[512,512]{1,0:T(8,128)}, f32[2,64]{1,0:T(2,128)}, f32[3,256,512]{2,1,0:T(8,128)}, f32[2,64]{1,0:T(2,128)}, /*...) custom-call(bf16[512,512]{1,0:T(8,128)(2,1)} %get-tuple-element.34.r, ...), custom_call_target="tpu_custom_call" | custom-call | tf_op jit(solution)/shard_map/results/pallas_call | solution.py:1243

commit v2 on v1

--- a/solution.py
+++ b/solution.py
@@ -758,11 +758,11 @@
 
     attention(0)
     attn_copy(0).start()
+    attention(1)
+    attn_copy(1).start()
     upto(needed[2])
     fc2_chunk(2)
     mid(fc2_p[1])
-    attention(1)
-    attn_copy(1).start()
     arrive("wd", "w2")
 
     class Line:
@@ -874,11 +874,11 @@
         dg[:, pl.ds(i * BK, BK)] = out.astype(BF16)
         den_p[i].start(0)
 
-    mid(fc2_p[2])
     for i in range(nt - 1):
         dense_chunk(i)
     out_rows(0)
     upto(needed[3])
+    mid(fc2_p[2])
     for k in range(nt):
         line_o.pair(k).wait()
     @pl.loop(0, nt - 1)

time: 174 us -> 174 us (level)
  no operation moved by 1% of the time
where the time goes in v2:
time: 174 us
  Pallas kernels  173 us (99%)
    pallas_call x1, Pallas kernels, per_device(): pl.pallas_call(functools.partial(block_kernel, pn, direct), out_shape=[ja...  168 us
    pallas_call x1, Pallas kernels, results(): pl.pallas_call(functools.partial(results_kernel, nq, direct), out_shape=[...  5.32 us

profile of v2, /device:TPU:0, one launch (start us, length us, event | category | flops | bytes accessed | tf_op | source)
XLA Modules:
  0.0 173.9 jit_solution(14383300488273374937)
XLA Ops:
  0.6 167.7 %block.1 = (bf16[512,512]{1,0:T(8,128)(2,1)}, f32[512,512]{1,0:T(8,128)}, f32[2,64]{1,0:T(2,128)}, f32[3,256,256]{2,1,0:T(8,128)}, f32[2,64]{1,0:T(2,128)}, /*in...) custom-call(bf16[512,512]{1,0:T(8,128)(2,1)} %refs_0_.1, ...), custom_call_target="tpu_custom_call" | custom-call | tf_op jit(solution)/shard_map/block/pallas_call | solution.py:1384
  168.4 5.3 %results.1 = (bf16[512,512]{1,0:T(8,128)(2,1)}, f32[512,512]{1,0:T(8,128)}, f32[2,64]{1,0:T(2,128)}, f32[3,256,512]{2,1,0:T(8,128)}, f32[2,64]{1,0:T(2,128)}, /*...) custom-call(bf16[512,512]{1,0:T(8,128)(2,1)} %get-tuple-element.34.r, ...), custom_call_target="tpu_custom_call" | custom-call | tf_op jit(solution)/shard_map/results/pallas_call | solution.py:1243
